TPU v7x, 256 devices: a whole 4x4x8 slice. The times are simulated.
256 devices in a mesh: grp: 16 (over z, core), reg: 16 (over y, x).
Axes of the slice: x: 4, y: 4, z: 8, core: 2. Of those that a mesh axis runs over, the one named last changes fastest.
Arguments:
- queries: bfloat16 [32768, 1536], P(('grp', 'reg')), parts along dimension 0, may hold values from -9 to 9
- keys_now: bfloat16 [32768, 1536], P(('grp', 'reg')), parts along dimension 0, may hold values from -9 to 9
- values_now: bfloat16 [32768, 1536], P(('grp', 'reg')), parts along dimension 0, may hold values from -6 to 6
- keys_stale: bfloat16 [32768, 1536], P(('grp', 'reg')), parts along dimension 0, may hold values from -9 to 9
- values_stale: bfloat16 [32768, 1536], P(('grp', 'reg')), parts along dimension 0, may hold values from -6 to 6
- neighbours: int32 [256, 8], P('grp'), parts along dimension 0, may hold values from -1 to 15, as said below
Outputs:
- attended: bfloat16 [32768, 1536], P(('grp', 'reg')), parts along dimension 0
There are 16 independent parts, one for each index of `grp`. A program takes and returns all parts, laid end to end along the dimension named above; each array names one. Nothing has to cross between parts.
Inputs may be any that keep to these rules, and one draw needn't show every extreme that they name: `neighbours`: row r holds first between 1 and 8 distinct region numbers other than r, then -1 in its remaining slots; some row holds 8 numbers.
All inputs are finite; a program needn't handle non-finite values.
Results may differ from a plain program's by a relative error of at most 0.0085.
Values may be sent and summed in bfloat16 or wider, within the bound.
A program may use at most 128 MiB of HBM per device.

v0:
```python
import jax
import jax.numpy as jnp
from jax import lax
from jax.sharding import PartitionSpec as P

HD = 128
HALO = 128


def with_halo(x, sides, width):
    for axis, dim in sides:
        count, length = (lax.axis_size(axis), x.shape[dim])
        up = [(i, (i + 1) % count) for i in range(count - 1)]
        down = [(j, i) for i, j in up]
        last = lax.slice_in_dim(x, length - width, length, axis=dim)
        initial = lax.slice_in_dim(x, 0, width, axis=dim)
        before = lax.ppermute(last, axis, up)
        after = lax.ppermute(initial, axis, down)
        x = jnp.concatenate([before, x, after], axis=dim)
    return x


def side_by_side(arrays, axis, dim, along):
    ends, at = ([], 0)
    for a in arrays[:-1]:
        at += a.shape[along]
        ends.append(at)
    both = jnp.concatenate(arrays, axis=along)
    return tuple(jnp.split(lax.all_gather(both, axis, axis=dim, tiled=True), ends, axis=along))


def block_partial(query_rows, key_rows, value_rows, key_valid):
    rows = query_rows.shape[0]
    count = key_rows.shape[0]
    heads = query_rows.shape[1] // HD
    query3 = query_rows.reshape(rows, heads, HD)
    key3 = key_rows.reshape(count, heads, HD)
    value3 = value_rows.reshape(count, heads, HD)
    scores = jnp.einsum("thd,shd->ths", query3, key3, preferred_element_type=jnp.float32) * HD ** (
        -0.5
    )
    if key_valid is not None:
        scores = jnp.where(key_valid[None, None, :], scores, -jnp.inf)
    peak = jnp.max(scores, axis=-1)
    weights = jnp.exp(scores - peak[..., None])
    total = jnp.sum(weights, axis=-1)
    numer = jnp.einsum(
        "ths,shd->thd", weights.astype(jnp.bfloat16), value3, preferred_element_type=jnp.float32
    )
    partial_out = (numer / total[..., None]).reshape(rows, heads * HD).astype(jnp.bfloat16)
    return (peak, total, partial_out)


def empty_partial(rows, width):
    heads = width // HD
    return (
        jnp.zeros((rows, heads), jnp.float32),
        jnp.zeros((rows, heads), jnp.float32),
        jnp.zeros((rows, width), jnp.bfloat16),
    )


def absorb(carry, piece, taken):
    top, denom, numer = carry
    peak, total, partial_out = piece
    rows, heads = top.shape
    new_top = jnp.where(taken, jnp.maximum(top, peak), top)
    keep = jnp.exp(top - new_top)
    fresh = jnp.exp(jnp.where(taken, peak, new_top) - new_top) * jnp.where(taken, total, 0.0)
    denom = denom * keep + fresh
    numer = numer * keep[..., None] + fresh[..., None] * partial_out.reshape(
        rows, heads, HD
    ).astype(jnp.float32)
    return (new_top, denom, numer)


def on_device(queries, keys_now, values_now, keys_stale, values_stale, neighbours):
    count = lax.axis_size("reg")
    region = lax.axis_index("reg")
    rows = queries.shape[0]
    width = queries.shape[1]
    heads = width // HD
    stacked = jnp.stack([keys_now, values_now])
    padded = with_halo(stacked, (("reg", 1),), HALO)
    span = rows + 2 * HALO
    position = jnp.arange(span, dtype=jnp.int32)
    valid = ((position >= HALO) | (region > 0)) & ((position < rows + HALO) | (region < count - 1))
    peak_local, total_local, out_local = block_partial(queries, padded[0], padded[1], valid)
    carry = (
        peak_local,
        total_local,
        out_local.reshape(rows, heads, HD).astype(jnp.float32) * total_local[..., None],
    )
    own_list = lax.dynamic_index_in_dim(neighbours, region, 0, keepdims=False)
    owners = jnp.arange(count, dtype=jnp.int32)
    member = jnp.any(own_list[:, None] == owners[None, :], axis=0)
    gathered_keys, gathered_values = side_by_side((keys_stale, values_stale), "reg", 0, 1)

    def visit(owner, state):
        taken = member[owner]

        def compute():
            key_rows = lax.dynamic_slice_in_dim(gathered_keys, owner * rows, rows, 0)
            value_rows = lax.dynamic_slice_in_dim(gathered_values, owner * rows, rows, 0)
            return block_partial(queries, key_rows, value_rows, None)

        piece = lax.cond(taken, compute, lambda: empty_partial(rows, width))
        return absorb(state, piece, taken)

    carry = lax.fori_loop(0, count, visit, carry)
    top, denom, numer = carry
    return (numer / denom[..., None]).reshape(rows, width).astype(jnp.bfloat16)


def solution(mesh):
    in_specs = (
        P(("grp", "reg"), None),
        P(("grp", "reg"), None),
        P(("grp", "reg"), None),
        P(("grp", "reg"), None),
        P(("grp", "reg"), None),
        P("grp", None),
    )
    out_specs = P(("grp", "reg"), None)
    return jax.shard_map(
        on_device, mesh=mesh, in_specs=in_specs, out_specs=out_specs, check_vma=False
    )
```

profile of v0, /device:TPU:72, one launch (start us, length us, event | category | flops | bytes accessed | tf_op | source)
XLA Modules:
  0.0 234.9 jit_solution(17577109386759798454)
XLA Ops:
  10.6 4.6 %collective-permute-start.1 = (bf16[2,128,1536]{1,2,0:T(8,128)(2,1)S(1)}, bf16[2,128,1536]{1,2,0:T(8,128)(2,1)S(1)}, u32[]{:S(2)}, u32[]{:S(2)}) collective-permute-start(bf16[2,128,1536]{1,2,0:T(8,128)(2,1)S(1)} %pad_maximum_fusion.1), channel_id=1, source_target_pairs={{1,0},{2,1},{3,2},{4,3},{5,4},{6,5},{7,6},{8,7},{9,8},{10,9},{11,1... | collective-permute-start | bytes 2359304 | tf_op jit(solution)/shard_map/ppermute | solution.py:18
  15.2 1.9 collective-permute-start
  18.6 17.5 %collective-permute-done.1 = bf16[2,128,1536]{1,2,0:T(8,128)(2,1)S(1)} collective-permute-done((bf16[2,128,1536]{1,2,0:T(8,128)(2,1)S(1)}, bf16[2,128,1536]{1,2,0:T(8,128)(2,1)S(1)}, u32[]{:S(2)}, u32[]{:S(2)}) %collective-permute-start.1) | collective-permute-done | bytes 786464 | tf_op jit(solution)/shard_map/ppermute | solution.py:18
  36.2 10.5 %collective-permute-done = bf16[2,128,1536]{1,2,0:T(8,128)(2,1)S(1)} collective-permute-done((bf16[2,128,1536]{1,2,0:T(8,128)(2,1)S(1)}, bf16[2,128,1536]{1,2,0:T(8,128)(2,1)S(1)}, u32[]{:S(2)}, u32[]{:S(2)}) %collective-permute-start) | collective-permute-done | bytes 786464 | tf_op jit(solution)/shard_map/ppermute | solution.py:17
  49.3 73.8 %all-gather.2.cloned.1.call-done = bf16[2048,3072]{0,1:T(8,128)(2,1)} async-done(((bf16[128,3072]{0,1:T(8,128)(2,1)}), bf16[2048,3072]{0,1:T(8,128)(2,1)}) %all-gather.2.cloned.1.call-update) | async-done | bytes 12582928 | tf_op jit(solution)/shard_map/all_gather | solution.py:29
  123.1 10.6 %fusion.30 = (bf16[2048,1536]{0,1:T(8,128)(2,1)}, bf16[2048,1536]{0,1:T(8,128)(2,1)}) fusion(bf16[2048,3072]{0,1:T(8,128)(2,1)} %all-gather.2.cloned.1.call-done), kind=kLoop, calls=%fused_computation.49 | loop fusion | bytes 25165824 | tf_op jit(solution)/shard_map/split | solution.py:29
  133.7 93.3 %while.17 = (s32[]{:T(128)}, f32[128,12]{0,1:T(8,128)S(1)}, f32[128,12]{0,1:T(8,128)S(1)}, f32[128,12,128]{0,2,1:T(8,128)S(1)}, pred[16]{0:T(512)(128)(4,1)S(1)}...) while((s32[]{:T(128)}, f32[128,12]{0,1:T(8,128)S(1)}, ...), condition=%wide.region_8.9_spmd, body=%wide.region_3.8_spmd.sunk | while | flops 103033344 | bytes 8349915 | solution.py:110
  135.0 4.5 %conditional.2 = (f32[128,12]{0,1:T(8,128)}, f32[128,12]{0,1:T(8,128)}, f32[128,12,128]{0,2,1:T(8,128)S(1)}) conditional(s32[]{:T(128)} %convert_element_type.63, () %tuple.53, (s32[]{:T(128)}, bf16[2048,1536]{0,1:T(8,128)(2,1)}, bf16[128,1536]{0,1:T(8,128)(2,1)S(1)}, bf16[2048,1536]{0,1:T(8,128)(2,1)}) %tuple.54), branch_computations={%region_4.4_spmd, %region_5.7_spmd} | conditional | flops 102429696 | bytes 5929034 | solution.py:107
  137.1 1.4 fusion.5
  139.5 1.4 multiply_add_fusion.4
  142.4 4.5 %conditional.2 = (f32[128,12]{0,1:T(8,128)}, f32[128,12]{0,1:T(8,128)}, f32[128,12,128]{0,2,1:T(8,128)S(1)}) conditional(s32[]{:T(128)} %convert_element_type.63, () %tuple.53, (s32[]{:T(128)}, bf16[2048,1536]{0,1:T(8,128)(2,1)}, bf16[128,1536]{0,1:T(8,128)(2,1)S(1)}, bf16[2048,1536]{0,1:T(8,128)(2,1)}) %tuple.54), branch_computations={%region_4.4_spmd, %region_5.7_spmd} | conditional | flops 102429696 | bytes 5929034 | solution.py:107
  144.6 1.4 fusion.5
  147.0 1.4 multiply_add_fusion.4
  149.9 4.5 %conditional.2 = (f32[128,12]{0,1:T(8,128)}, f32[128,12]{0,1:T(8,128)}, f32[128,12,128]{0,2,1:T(8,128)S(1)}) conditional(s32[]{:T(128)} %convert_element_type.63, () %tuple.53, (s32[]{:T(128)}, bf16[2048,1536]{0,1:T(8,128)(2,1)}, bf16[128,1536]{0,1:T(8,128)(2,1)S(1)}, bf16[2048,1536]{0,1:T(8,128)(2,1)}) %tuple.54), branch_computations={%region_4.4_spmd, %region_5.7_spmd} | conditional | flops 102429696 | bytes 5929034 | solution.py:107
  152.1 1.4 fusion.5
  154.5 1.4 multiply_add_fusion.4
  165.8 4.5 %conditional.2 = (f32[128,12]{0,1:T(8,128)}, f32[128,12]{0,1:T(8,128)}, f32[128,12,128]{0,2,1:T(8,128)S(1)}) conditional(s32[]{:T(128)} %convert_element_type.63, () %tuple.53, (s32[]{:T(128)}, bf16[2048,1536]{0,1:T(8,128)(2,1)}, bf16[128,1536]{0,1:T(8,128)(2,1)S(1)}, bf16[2048,1536]{0,1:T(8,128)(2,1)}) %tuple.54), branch_computations={%region_4.4_spmd, %region_5.7_spmd} | conditional | flops 102429696 | bytes 5929034 | solution.py:107
  167.9 1.4 fusion.5
  170.3 1.4 multiply_add_fusion.4
  174.5 1.4 multiply_add_fusion.4
  181.6 4.5 %conditional.2 = (f32[128,12]{0,1:T(8,128)}, f32[128,12]{0,1:T(8,128)}, f32[128,12,128]{0,2,1:T(8,128)S(1)}) conditional(s32[]{:T(128)} %convert_element_type.63, () %tuple.53, (s32[]{:T(128)}, bf16[2048,1536]{0,1:T(8,128)(2,1)}, bf16[128,1536]{0,1:T(8,128)(2,1)S(1)}, bf16[2048,1536]{0,1:T(8,128)(2,1)}) %tuple.54), branch_computations={%region_4.4_spmd, %region_5.7_spmd} | conditional | flops 102429696 | bytes 5929034 | solution.py:107
  183.8 1.4 fusion.5
  186.2 1.4 multiply_add_fusion.4
  197.5 4.5 %conditional.2 = (f32[128,12]{0,1:T(8,128)}, f32[128,12]{0,1:T(8,128)}, f32[128,12,128]{0,2,1:T(8,128)S(1)}) conditional(s32[]{:T(128)} %convert_element_type.63, () %tuple.53, (s32[]{:T(128)}, bf16[2048,1536]{0,1:T(8,128)(2,1)}, bf16[128,1536]{0,1:T(8,128)(2,1)S(1)}, bf16[2048,1536]{0,1:T(8,128)(2,1)}) %tuple.54), branch_computations={%region_4.4_spmd, %region_5.7_spmd} | conditional | flops 102429696 | bytes 5929034 | solution.py:107
  199.7 1.4 fusion.5
  202.1 1.4 multiply_add_fusion.4
  213.4 4.5 %conditional.2 = (f32[128,12]{0,1:T(8,128)}, f32[128,12]{0,1:T(8,128)}, f32[128,12,128]{0,2,1:T(8,128)S(1)}) conditional(s32[]{:T(128)} %convert_element_type.63, () %tuple.53, (s32[]{:T(128)}, bf16[2048,1536]{0,1:T(8,128)(2,1)}, bf16[128,1536]{0,1:T(8,128)(2,1)S(1)}, bf16[2048,1536]{0,1:T(8,128)(2,1)}) %tuple.54), branch_computations={%region_4.4_spmd, %region_5.7_spmd} | conditional | flops 102429696 | bytes 5929034 | solution.py:107
  215.5 1.4 fusion.5
  217.9 1.4 multiply_add_fusion.4
  220.8 4.5 %conditional.2 = (f32[128,12]{0,1:T(8,128)}, f32[128,12]{0,1:T(8,128)}, f32[128,12,128]{0,2,1:T(8,128)S(1)}) conditional(s32[]{:T(128)} %convert_element_type.63, () %tuple.53, (s32[]{:T(128)}, bf16[2048,1536]{0,1:T(8,128)(2,1)}, bf16[128,1536]{0,1:T(8,128)(2,1)S(1)}, bf16[2048,1536]{0,1:T(8,128)(2,1)}) %tuple.54), branch_computations={%region_4.4_spmd, %region_5.7_spmd} | conditional | flops 102429696 | bytes 5929034 | solution.py:107
  223.0 1.4 fusion.5
  225.4 1.4 multiply_add_fusion.4
  (120 shorter events, 78.0 us)
Async XLA Ops:
  6.5 11.8 %copy-start = (s32[16,8]{0,1:T(8,128)S(1)}, s32[16,8]{0,1:T(8,128)}, u32[]{:S(2)}) copy-start(s32[16,8]{0,1:T(8,128)} %param.15) | copy-start | bytes 1540
  6.5 3.5 %copy-start.1 = (bf16[128,1536]{1,0:T(8,128)(2,1)S(1)}, bf16[128,1536]{1,0:T(8,128)(2,1)}, u32[]{:S(2)}) copy-start(bf16[128,1536]{1,0:T(8,128)(2,1)} %param.11) | copy-start | bytes 1179652
  6.5 3.8 %copy-start.2 = (bf16[128,1536]{1,0:T(8,128)(2,1)S(1)}, bf16[128,1536]{1,0:T(8,128)(2,1)}, u32[]{:S(2)}) copy-start(bf16[128,1536]{1,0:T(8,128)(2,1)} %param.12) | copy-start | bytes 1179652
  6.5 116.5 %all-gather.2.cloned.1.call-start = ((), (), s32[]{:S(2)}) async-start(), calls=%async_computation | async-start | bytes 13369344 | tf_op jit(solution)/shard_map/all_gather | solution.py:29
  10.6 25.6 %collective-permute-start.1 = (bf16[2,128,1536]{1,2,0:T(8,128)(2,1)S(1)}, bf16[2,128,1536]{1,2,0:T(8,128)(2,1)S(1)}, u32[]{:S(2)}, u32[]{:S(2)}) collective-permute-start(bf16[2,128,1536]{1,2,0:T(8,128)(2,1)S(1)} %pad_maximum_fusion.1), channel_id=1, source_target_pairs={{1,0},{2,1},{3,2},{4,3},{5,4},{6,5},{7,6},{8,7},{9,8},{10,9},{11,1... | collective-permute-start | bytes 2359304 | tf_op jit(solution)/shard_map/ppermute | solution.py:18
  15.2 31.5 %collective-permute-start = (bf16[2,128,1536]{1,2,0:T(8,128)(2,1)S(1)}, bf16[2,128,1536]{1,2,0:T(8,128)(2,1)S(1)}, u32[]{:S(2)}, u32[]{:S(2)}) collective-permute-start(bf16[2,128,1536]{1,2,0:T(8,128)(2,1)S(1)} %pad_maximum_fusion.1), channel_id=1, source_target_pairs={{0,1},{1,2},{2,3},{3,4},{4,5},{5,6},{6,7},{7,8},{8,9},{9,10},{10,1... | collective-permute-start | bytes 2359304 | tf_op jit(solution)/shard_map/ppermute | solution.py:17
Sparse Core Ops, SparseCore 0:
  10.2 112.8 all-gather.1
where the time goes:
time: 238 us; the launch traced here: 235 us
  waiting for transfers between devices  102 us (43%)
  local copies, waits for them, and re-layouts  45.5 us (19%)
  other arithmetic  39.7 us (17%)
  matrix products  16.8 us (7%)
  between operations  13.5 us (6%)
  loops' own time  11.1 us (5%)
  starting transfers between devices  6.48 us (3%)
    all_gather x1, waiting for transfers between devices, side_by_side(): lax.all_gather(both, axis, axis=dim, tiled=True)  73.8 us
    add x16, other arithmetic, absorb(): denom = denom * keep + fresh  21.7 us
    ppermute x1, waiting for transfers between devices, with_halo(): after = lax.ppermute(initial, axis, down)  17.5 us
    reduce_sum x9, other arithmetic, block_partial(): total = jnp.sum(weights, axis=-1)  11.9 us
    another operation x1, loops' own time, on_device(): carry = lax.fori_loop(0, count, visit, carry)  10.7 us
    split x1, local copies, waits for them, and re-layouts, side_by_side(): jnp.split(lax.all_gather(both, axis, axis=dim, tiled=True), ends, axis=al...  10.6 us
    ppermute x1, waiting for transfers between devices, with_halo(): before = lax.ppermute(last, axis, up)  10.5 us
    dynamic_slice x16, local copies, waits for them, and re-layouts, visit(): taken = member[owner]  9.83 us
  transfers between devices with their start and end apart: 3, of which 3 were waited for; matrix products, arithmetic and copies ran while one was open for 2% of the time, Pallas kernels for 0%

commit v1 on v0

v1 whole, which is shorter than its diff:
```python
import functools

import jax
import jax.numpy as jnp
from jax import lax
from jax.experimental import pallas as pl
from jax.experimental.pallas import tpu as pltpu
from jax.sharding import PartitionSpec as P

HD = 128
MESH = pl.DeviceIdType.MESH
LOG2E = 1.4426950408889634
LOW = -1e30
ORDER = (
    (0, 1), (0, 3), (1, 0), (3, 0), (1, 1), (3, 3), (1, 3), (3, 1),
    (2, 0), (0, 2), (2, 1), (3, 2), (2, 3), (1, 2), (2, 2),
)


def kernel(side, slots, nb_ref, q_ref, ks_ref, kn_ref, vs_ref, vn_ref, out_ref,
           stage, in_q, in_ks, in_kn, in_vs, in_vn, ps, pn, mb, lb, osum, outbox,
           load_sem, send_sem, recv_sem, osend_sem, orecv_sem):
    n = side * side
    per = side - 1
    heads = per * side
    rows = q_ref.shape[0]
    core = lax.rem(lax.axis_index("grp"), 2)
    me = lax.axis_index("reg")
    y, x = me // side, lax.rem(me, side)
    scale = HD ** -0.5 * LOG2E

    def place(dy, dx):
        yy, xx = lax.rem(y + dy, side), lax.rem(x + dx, side)
        kk = lax.rem(xx + yy + 2 * core, side)
        return yy * side + xx, yy * per + kk, kk < per

    _, my_head, active = place(0, 0)
    args = (q_ref, ks_ref, kn_ref, vs_ref, vn_ref)
    inbox = (in_q, in_ks, in_kn, in_vs, in_vn)

    def cols(h):
        return pl.ds(pl.multiple_of(h * HD, HD), HD)

    for t, ref in enumerate(args):
        pltpu.make_async_copy(ref, stage.at[t], load_sem.at[t]).start()

    barrier = pltpu.get_barrier_semaphore()
    for o in range(1, n):
        pl.semaphore_signal(barrier, inc=1, device_id={"reg": lax.rem(me + o, n)}, device_id_type=MESH)

    @pl.when(active)
    def _():
        for t, ref in enumerate(args):
            pltpu.make_async_copy(ref.at[:, cols(my_head)], inbox[t].at[me], recv_sem.at[t]).start()

    pl.semaphore_wait(barrier, n - 1)

    for t, ref in enumerate(args):
        pltpu.make_async_copy(ref, stage.at[t], load_sem.at[t]).wait()
        for dy, dx in ORDER:
            dev, head, owns = place(dy, dx)

            @pl.when(owns)
            def _():
                pltpu.make_async_remote_copy(
                    src_ref=stage.at[t, :, cols(head)],
                    dst_ref=inbox[t].at[me],
                    send_sem=send_sem.at[t],
                    recv_sem=recv_sem.at[t],
                    device_id={"reg": dev},
                    device_id_type=MESH,
                ).start()

    def arrived(t):
        pltpu.make_async_copy(inbox[t], inbox[t], recv_sem.at[t]).wait()

    def softmax_parts(scores):
        peak = jnp.max(scores, axis=-1, keepdims=True)
        weights = jnp.exp2((scores - peak) * scale)
        total = jnp.sum(weights, axis=-1, keepdims=True)
        return peak, weights, total

    @pl.when(active)
    def _():
        arrived(0)
        arrived(1)

        def stale_scores(r, _):
            q = in_q[r]
            idx = [nb_ref[s, r] for s in range(slots)]
            keys = jnp.concatenate([in_ks[jnp.maximum(i, 0)] for i in idx], axis=0)
            sc = lax.dot_general(q, keys, (((1,), (1,)), ((), ())), preferred_element_type=jnp.float32)
            sc = jnp.concatenate(
                [jnp.where(i >= 0, sc[:, s * rows:(s + 1) * rows], LOW) for s, i in enumerate(idx)], axis=1)
            peak, weights, total = softmax_parts(sc)
            ps[r] = weights.astype(jnp.bfloat16)
            mb[r] = jnp.broadcast_to(peak, (rows, HD))
            lb[r] = jnp.broadcast_to(total, (rows, HD))
            return 0

        lax.fori_loop(0, n, stale_scores, 0)
        arrived(2)

        def local_scores(r, _):
            q = in_q[r]
            keys = jnp.concatenate(
                [in_kn[jnp.maximum(r - 1, 0)], in_kn[r], in_kn[jnp.minimum(r + 1, n - 1)]], axis=0)
            sc = lax.dot_general(q, keys, (((1,), (1,)), ((), ())), preferred_element_type=jnp.float32)
            sc = jnp.concatenate([
                jnp.where(r > 0, sc[:, :rows], LOW),
                sc[:, rows:2 * rows],
                jnp.where(r < n - 1, sc[:, 2 * rows:], LOW)], axis=1)
            peak, weights, total = softmax_parts(sc)
            peak_s, total_s = mb[r], lb[r]
            peak = jnp.broadcast_to(peak, (rows, HD))
            top = jnp.maximum(peak, peak_s)
            keep_n = jnp.exp2((peak - top) * scale)
            keep_s = jnp.exp2((peak_s - top) * scale)
            inv = 1.0 / (keep_n * total + keep_s * total_s)
            lb[r] = keep_s * inv
            wn = keep_n * inv
            pn[r] = (weights * jnp.concatenate([wn, wn, wn], axis=1)).astype(jnp.bfloat16)
            return 0

        lax.fori_loop(0, n, local_scores, 0)
        arrived(3)

        def stale_values(r, _):
            values = jnp.concatenate(
                [in_vs[jnp.maximum(nb_ref[s, r], 0)] for s in range(slots)], axis=0)
            osum[r] = lb[r] * jnp.dot(ps[r], values, preferred_element_type=jnp.float32)
            return 0

        lax.fori_loop(0, n, stale_values, 0)
        arrived(4)

        def tile(r):
            values = jnp.concatenate(
                [in_vn[jnp.maximum(r - 1, 0)], in_vn[r], in_vn[jnp.minimum(r + 1, n - 1)]], axis=0)
            return (osum[r] + jnp.dot(pn[r], values, preferred_element_type=jnp.float32)).astype(jnp.bfloat16)

        def finish(o, _):
            r = lax.rem(me + o, n)
            outbox[r] = tile(r)
            pltpu.make_async_remote_copy(
                src_ref=outbox.at[r],
                dst_ref=out_ref.at[:, cols(my_head)],
                send_sem=osend_sem,
                recv_sem=orecv_sem,
                device_id={"reg": r},
                device_id_type=MESH,
            ).start()
            return 0

        lax.fori_loop(1, n, finish, 0)
        out_ref[:, cols(my_head)] = tile(me)

    def spent(count):
        for t in range(len(args)):
            part = stage.at[t, :, pl.ds(0, count * HD)]
            pltpu.make_async_copy(part, part, send_sem.at[t]).wait()
        got = out_ref.at[:, pl.ds(0, count * HD)]
        pltpu.make_async_copy(got, got, orecv_sem).wait()

    @pl.when(active)
    def _():
        spent(heads - 1)
        sent = outbox.at[pl.ds(0, n - 1)]
        pltpu.make_async_copy(sent, sent, osend_sem).wait()

    @pl.when(jnp.logical_not(active))
    def _():
        spent(heads)


def solution(mesh):
    n = mesh.shape["reg"]
    side = 4
    assert side * side == n

    def on_device(queries, keys_now, values_now, keys_stale, values_stale, neighbours):
        rows, width = queries.shape
        slots = neighbours.shape[1]
        any_spec = pl.BlockSpec(memory_space=pl.ANY)
        return pl.pallas_call(
            functools.partial(kernel, side, slots),
            out_shape=jax.ShapeDtypeStruct((rows, width), jnp.bfloat16),
            in_specs=[pl.BlockSpec(memory_space=pltpu.SMEM)] + [any_spec] * 5,
            out_specs=pl.BlockSpec(memory_space=pltpu.VMEM),
            scratch_shapes=[
                pltpu.VMEM((5, rows, width), jnp.bfloat16),
            ] + [pltpu.VMEM((n, rows, HD), jnp.bfloat16)] * 5 + [
                pltpu.VMEM((n, rows, slots * rows), jnp.bfloat16),
                pltpu.VMEM((n, rows, 3 * rows), jnp.bfloat16),
                pltpu.VMEM((n, rows, HD), jnp.float32),
                pltpu.VMEM((n, rows, HD), jnp.float32),
                pltpu.VMEM((n, rows, HD), jnp.float32),
                pltpu.VMEM((n, rows, HD), jnp.bfloat16),
                pltpu.SemaphoreType.DMA((5,)),
                pltpu.SemaphoreType.DMA((5,)),
                pltpu.SemaphoreType.DMA((5,)),
                pltpu.SemaphoreType.DMA,
                pltpu.SemaphoreType.DMA,
            ],
            compiler_params=pltpu.CompilerParams(collective_id=0, has_side_effects=True),
        )(neighbours.T, queries, keys_stale, keys_now, values_stale, values_now)

    in_specs = (P(("grp", "reg"), None),) * 5 + (P("grp", None),)
    return jax.shard_map(
        on_device, mesh=mesh, in_specs=in_specs, out_specs=P(("grp", "reg"), None), check_vma=False
    )
```

time: 238 us -> 60.9 us (0.26)
  the two profiles are of different devices: /device:TPU:72 before, /device:TPU:192 now
where the time goes in v1:
time: 60.9 us; the launch traced here: 60.8 us
  Pallas kernels  59 us (97%)
  local copies, waits for them, and re-layouts  1.77 us (3%)
    pallas_call x1, Pallas kernels, on_device(): pl.pallas_call(functools.partial(kernel, side, slots), out_shape=jax.Shap...  59 us
    unnamed x1, local copies, waits for them, and re-layouts  1.77 us

profile of v1, /device:TPU:192, one launch (start us, length us, event | category | flops | bytes accessed | tf_op | source)
XLA Modules:
  0.0 60.8 jit_solution(1204540376202801541)
XLA Ops:
  0.0 59.0 %shard_map.64 = bf16[128,1536]{1,0:T(8,128)(2,1)} custom-call(s32[8,16]{1,0:T(8,128)} %bitcast.1, bf16[128,1536]{1,0:T(8,128)(2,1)} %q_ref.1, bf16[128,1536]{1,0:T(8,128)(2,1)} %ks_ref.1, bf16[128,1536]{1,0:T(8,128)(2,1)} %kn_ref.1, bf16[128,1536]{1,0:T(8,128)(2,1)} %vs_ref.1, bf16[128,1536]{1,0:T(8,128)(2,1)} %vn_ref.1), custom_call_target="tpu_custom_call" | custom-call | tf_op jit(solution)/shard_map/pallas_call | solution.py:185
  59.0 1.8 %copy.8 = bf16[128,1536]{1,0:T(8,128)(2,1)} copy(bf16[128,1536]{1,0:T(8,128)(2,1)} %shard_map.64) | data formatting | bytes 786432

commit v2 on v1

v2 whole, which is shorter than its diff:
```python
import functools

import jax
import jax.numpy as jnp
from jax import lax
from jax.experimental import pallas as pl
from jax.experimental.pallas import tpu as pltpu
from jax.sharding import PartitionSpec as P

HD = 128
MESH = pl.DeviceIdType.MESH
LOG2E = 1.4426950408889634
LOW = -1e30
GROUP = 4
Q, KS, KN, VS, VN = range(5)
ORDER = (
    (0, 1), (0, 3), (1, 0), (3, 0), (1, 1), (3, 3), (1, 3), (3, 1),
    (2, 0), (0, 2), (2, 1), (3, 2), (2, 3), (1, 2), (2, 2),
)


def kernel(side, slots, nb_ref, q_ref, ks_ref, kn_ref, vs_ref, vn_ref, out_ref,
           stage, in_q, in_ks, in_kn, in_vs, in_vn, ps, pn, mb, lb, osum, outbox,
           load_sem, send_sem, recv_sem, fsend_sem, frecv_sem, osend_sem, orecv_sem):
    n = side * side
    half = n // 2
    rows = q_ref.shape[0]
    core = lax.rem(lax.axis_index("grp"), 2)
    me = lax.axis_index("reg")
    y, x = me // side, lax.rem(me, side)
    part = y // 2
    scale = HD ** -0.5 * LOG2E
    args = (q_ref, ks_ref, kn_ref, vs_ref, vn_ref)
    inbox = (in_q, in_ks, in_kn, in_vs, in_vn)

    def role(yy, xx):
        whole = lax.rem(xx + core, 2) == 0
        outer = (yy // (side - 1) + (side - 1 - yy) // (side - 1)).astype(jnp.int32)
        return whole, jnp.where(whole, yy * 2 + xx // 2, n // 2 + 2 * outer + xx // 2)

    whole, my_head = role(y, x)
    shared = jnp.logical_not(whole)
    partner = (side - 1 - y) * side + x
    edge = jnp.logical_or(me == half - 1, me == half)
    first = jnp.where(whole, 0, part * half)
    count = jnp.where(whole, n, half)

    def cols(h):
        return pl.ds(pl.multiple_of(h * HD, HD), HD)

    for t, ref in enumerate(args):
        pltpu.make_async_copy(ref, stage.at[t], load_sem.at[t]).start()
    for t, ref in enumerate(args):
        pltpu.make_async_copy(ref.at[:, cols(my_head)], inbox[t].at[me], recv_sem.at[t]).start()

    barrier = pltpu.get_barrier_semaphore()
    for o in range(1, n):
        pl.semaphore_signal(barrier, inc=1, device_id={"reg": lax.rem(me + o, n)}, device_id_type=MESH)
    pl.semaphore_wait(barrier, n - 1)

    def send(t):
        pltpu.make_async_copy(args[t], stage.at[t], load_sem.at[t]).wait()
        for dy, dx in ORDER:
            yy, xx = lax.rem(y + dy, side), lax.rem(x + dx, side)
            takes, head = role(yy, xx)
            takes = jnp.logical_or(takes, yy // 2 == part)
            if t in (KN, VN):
                takes = jnp.logical_or(takes, edge)

            @pl.when(takes)
            def _():
                pltpu.make_async_remote_copy(
                    src_ref=stage.at[t, :, cols(head)],
                    dst_ref=inbox[t].at[me],
                    send_sem=send_sem.at[t],
                    recv_sem=recv_sem.at[t],
                    device_id={"reg": yy * side + xx},
                    device_id_type=MESH,
                ).start()

    def wait(sem, tiles):
        some = in_q.at[pl.ds(0, tiles)]
        pltpu.make_async_copy(some, some, sem).wait()

    most = n - 1 - side

    def sent(t):
        if t in (KN, VN):
            @pl.when(edge)
            def _():
                wait(send_sem.at[t], n - 1)

            @pl.when(jnp.logical_not(edge))
            def _():
                wait(send_sem.at[t], most)
        else:
            wait(send_sem.at[t], most)

    def arrived(t):
        @pl.when(whole)
        def _():
            wait(recv_sem.at[t], n)

        @pl.when(shared)
        def _():
            wait(recv_sem.at[t], half + 1 if t in (KN, VN) else half)

    def forward(t):
        mine = inbox[t].at[pl.ds(part * half, half)]
        return pltpu.make_async_remote_copy(
            src_ref=mine,
            dst_ref=mine,
            send_sem=fsend_sem.at[t // 2],
            recv_sem=frecv_sem.at[t // 2],
            device_id={"reg": partner},
            device_id_type=MESH,
        )

    def pass_on(t):
        arrived(t)

        @pl.when(shared)
        def _():
            forward(t).start()

    def passed(t):
        @pl.when(shared)
        def _():
            wait(frecv_sem.at[t // 2], half)

    send(KS)
    send(Q)
    sent(KS)
    send(KN)
    pass_on(KS)
    sent(Q)
    send(VS)
    arrived(Q)
    passed(KS)

    def softmax_parts(scores):
        peak = jnp.max(scores, axis=-1, keepdims=True)
        weights = jnp.exp2((scores - peak) * scale)
        total = jnp.sum(weights, axis=-1, keepdims=True)
        return peak, weights, total

    def each(one, *outs):
        def step(i, _):
            at = [first + i * GROUP + k for k in range(GROUP)]
            got = [one(r) for r in at]
            for r, values in zip(at, got):
                for ref, value in zip(outs, values):
                    ref[r] = value
            return 0

        lax.fori_loop(0, count // GROUP, step, 0)

    def stale_scores(r):
        idx = [nb_ref[s, r] for s in range(slots)]
        keys = jnp.concatenate([in_ks[jnp.maximum(i, 0)] for i in idx], axis=0)
        sc = lax.dot_general(in_q[r], keys, (((1,), (1,)), ((), ())), preferred_element_type=jnp.float32)
        sc = jnp.concatenate(
            [jnp.where(i >= 0, sc[:, s * rows:(s + 1) * rows], LOW) for s, i in enumerate(idx)], axis=1)
        peak, weights, total = softmax_parts(sc)
        return weights.astype(jnp.bfloat16), jnp.broadcast_to(peak, (rows, HD)), jnp.broadcast_to(total, (rows, HD))

    each(stale_scores, ps, mb, lb)
    sent(KN)
    send(VN)
    pass_on(VS)
    arrived(KN)

    def around(ref, r):
        return jnp.concatenate([ref[jnp.maximum(r - 1, 0)], ref[r], ref[jnp.minimum(r + 1, n - 1)]], axis=0)

    def local_scores(r):
        sc = lax.dot_general(
            in_q[r], around(in_kn, r), (((1,), (1,)), ((), ())), preferred_element_type=jnp.float32)
        sc = jnp.concatenate([
            jnp.where(r > 0, sc[:, :rows], LOW),
            sc[:, rows:2 * rows],
            jnp.where(r < n - 1, sc[:, 2 * rows:], LOW)], axis=1)
        peak, weights, total = softmax_parts(sc)
        peak_s, total_s = mb[r], lb[r]
        peak = jnp.broadcast_to(peak, (rows, HD))
        top = jnp.maximum(peak, peak_s)
        keep_n = jnp.exp2((peak - top) * scale)
        keep_s = jnp.exp2((peak_s - top) * scale)
        inv = 1.0 / (keep_n * total + keep_s * total_s)
        wn = keep_n * inv
        return (weights * jnp.concatenate([wn, wn, wn], axis=1)).astype(jnp.bfloat16), keep_s * inv

    each(local_scores, pn, lb)
    passed(VS)

    def stale_values(r):
        values = jnp.concatenate([in_vs[jnp.maximum(nb_ref[s, r], 0)] for s in range(slots)], axis=0)
        return (lb[r] * jnp.dot(ps[r], values, preferred_element_type=jnp.float32),)

    each(stale_values, osum)
    arrived(VN)

    def tile(r):
        return (osum[r] + jnp.dot(pn[r], around(in_vn, r), preferred_element_type=jnp.float32)).astype(jnp.bfloat16)

    def finish(o, _):
        r = first + lax.rem(me - first + o, count)
        outbox[r] = tile(r)
        pltpu.make_async_remote_copy(
            src_ref=outbox.at[r],
            dst_ref=out_ref.at[:, cols(my_head)],
            send_sem=osend_sem,
            recv_sem=orecv_sem,
            device_id={"reg": r},
            device_id_type=MESH,
        ).start()
        return 0

    lax.fori_loop(1, count, finish, 0)
    out_ref[:, cols(my_head)] = tile(me)

    sent(VS)
    sent(VN)

    @pl.when(whole)
    def _():
        wait(osend_sem, n - 1)

    @pl.when(shared)
    def _():
        wait(osend_sem, half - 1)
        wait(fsend_sem.at[0], half)
        wait(fsend_sem.at[1], half)

    wait(orecv_sem, most)


def solution(mesh):
    n = mesh.shape["reg"]
    side = 4
    assert side * side == n

    def on_device(queries, keys_now, values_now, keys_stale, values_stale, neighbours):
        rows, width = queries.shape
        slots = neighbours.shape[1]
        assert width == (n - side) * HD
        any_spec = pl.BlockSpec(memory_space=pl.ANY)
        dma = pltpu.SemaphoreType.DMA
        return pl.pallas_call(
            functools.partial(kernel, side, slots),
            out_shape=jax.ShapeDtypeStruct((rows, width), jnp.bfloat16),
            in_specs=[pl.BlockSpec(memory_space=pltpu.SMEM)] + [any_spec] * 5,
            out_specs=pl.BlockSpec(memory_space=pltpu.VMEM),
            scratch_shapes=[pltpu.VMEM((5, rows, width), jnp.bfloat16)]
            + [pltpu.VMEM((n, rows, HD), jnp.bfloat16)] * 5
            + [
                pltpu.VMEM((n, rows, slots * rows), jnp.bfloat16),
                pltpu.VMEM((n, rows, 3 * rows), jnp.bfloat16),
                pltpu.VMEM((n, rows, HD), jnp.float32),
                pltpu.VMEM((n, rows, HD), jnp.float32),
                pltpu.VMEM((n, rows, HD), jnp.float32),
                pltpu.VMEM((n, rows, HD), jnp.bfloat16),
                dma((5,)), dma((5,)), dma((5,)), dma((2,)), dma((2,)), dma, dma,
            ],
            compiler_params=pltpu.CompilerParams(collective_id=0, has_side_effects=True),
        )(neighbours.T, queries, keys_stale, keys_now, values_stale, values_now)

    in_specs = (P(("grp", "reg"), None),) * 5 + (P("grp", None),)
    return jax.shard_map(
        on_device, mesh=mesh, in_specs=in_specs, out_specs=P(("grp", "reg"), None), check_vma=False
    )
```

time: 60.9 us -> 44 us (0.72)
  the two profiles are of different devices: /device:TPU:192 before, /device:TPU:64 now
where the time goes in v2:
time: 44 us; the launch traced here: 43.9 us
  Pallas kernels  42.1 us (96%)
  local copies, waits for them, and re-layouts  1.77 us (4%)
    pallas_call x1, Pallas kernels, on_device(): pl.pallas_call(functools.partial(kernel, side, slots), out_shape=jax.Shap...  42.1 us
    unnamed x1, local copies, waits for them, and re-layouts  1.77 us

profile of v2, /device:TPU:64, one launch (start us, length us, event | category | flops | bytes accessed | tf_op | source)
XLA Modules:
  0.0 43.9 jit_solution(14604805958626952530)
XLA Ops:
  0.0 42.1 %shard_map.64 = bf16[128,1536]{1,0:T(8,128)(2,1)} custom-call(s32[8,16]{1,0:T(8,128)} %bitcast.1, bf16[128,1536]{1,0:T(8,128)(2,1)} %q_ref.1, bf16[128,1536]{1,0:T(8,128)(2,1)} %ks_ref.1, bf16[128,1536]{1,0:T(8,128)(2,1)} %kn_ref.1, bf16[128,1536]{1,0:T(8,128)(2,1)} %vs_ref.1, bf16[128,1536]{1,0:T(8,128)(2,1)} %vn_ref.1), custom_call_target="tpu_custom_call" | custom-call | tf_op jit(solution)/shard_map/pallas_call | solution.py:249
  42.1 1.8 %copy.8 = bf16[128,1536]{1,0:T(8,128)(2,1)} copy(bf16[128,1536]{1,0:T(8,128)(2,1)} %shard_map.64) | data formatting | bytes 786432

commit v3 on v2

--- a/solution.py
+++ b/solution.py
@@ -262,8 +262,8 @@
                 pltpu.VMEM((n, rows, HD), jnp.bfloat16),
                 dma((5,)), dma((5,)), dma((5,)), dma((2,)), dma((2,)), dma, dma,
             ],
-            compiler_params=pltpu.CompilerParams(collective_id=0, has_side_effects=True),
-        )(neighbours.T, queries, keys_stale, keys_now, values_stale, values_now)
+            compiler_params=pltpu.CompilerParams(collective_id=0, has_side_effects=True, vmem_limit_bytes=20 << 20),
+        )(pltpu.with_memory_space_constraint(neighbours.T, pltpu.HBM), *[pltpu.with_memory_space_constraint(a, pltpu.HBM) for a in (queries, keys_stale, keys_now, values_stale, values_now)])
 
     in_specs = (P(("grp", "reg"), None),) * 5 + (P("grp", None),)
     return jax.shard_map(

time: 44 us -> 42.2 us (0.959)
  the two profiles are of different devices: /device:TPU:64 before, /device:TPU:192 now
where the time goes in v3:
time: 42.2 us; the launch traced here: 42.1 us
  Pallas kernels  41.3 us (98%)
  local copies, waits for them, and re-layouts  0.75 us (2%)
    pallas_call x1, Pallas kernels, on_device(): pl.pallas_call(functools.partial(kernel, side, slots), out_shape=jax.Shap...  41.3 us

profile of v3, /device:TPU:192, one launch (start us, length us, event | category | flops | bytes accessed | tf_op | source)
XLA Modules:
  0.0 42.1 jit_solution(15722029205871275335)
XLA Ops:
  0.0 41.3 %shard_map.64 = bf16[128,1536]{1,0:T(8,128)(2,1)S(1)} custom-call(s32[8,16]{1,0:T(8,128)} %bitcast.1, bf16[128,1536]{1,0:T(8,128)(2,1)} %q_ref.1, bf16[128,1536]{1,0:T(8,128)(2,1)} %ks_ref.1, bf16[128,1536]{1,0:T(8,128)(2,1)} %kn_ref.1, bf16[128,1536]{1,0:T(8,128)(2,1)} %vs_ref.1, bf16[128,1536]{1,0:T(8,128)(2,1)} %vn_ref.1), custom_call_target="tpu_custom_call" | custom-call | tf_op jit(solution)/shard_map/pallas_call | solution.py:249
  41.4 0.7 %copy.8 = bf16[128,1536]{1,0:T(8,128)(2,1)} copy(bf16[128,1536]{1,0:T(8,128)(2,1)S(1)} %shard_map.64) | data formatting | bytes 786432

commit v4 on v3

--- a/solution.py
+++ b/solution.py
@@ -17,11 +17,12 @@
     (0, 1), (0, 3), (1, 0), (3, 0), (1, 1), (3, 3), (1, 3), (3, 1),
     (2, 0), (0, 2), (2, 1), (3, 2), (2, 3), (1, 2), (2, 2),
 )
+FURTHER = ((1, 1), (2, 1), (2, 2))
 
 
 def kernel(side, slots, nb_ref, q_ref, ks_ref, kn_ref, vs_ref, vn_ref, out_ref,
            stage, in_q, in_ks, in_kn, in_vs, in_vn, ps, pn, mb, lb, osum, outbox,
-           load_sem, send_sem, recv_sem, fsend_sem, frecv_sem, osend_sem, orecv_sem):
+           load_sem, send_sem, recv_sem, fsend_sem, frecv_sem, osend_sem, orecv_sem, greet_sem):
     n = side * side
     half = n // 2
     rows = q_ref.shape[0]
@@ -53,14 +54,19 @@
     for t, ref in enumerate(args):
         pltpu.make_async_copy(ref.at[:, cols(my_head)], inbox[t].at[me], recv_sem.at[t]).start()
 
-    barrier = pltpu.get_barrier_semaphore()
-    for o in range(1, n):
-        pl.semaphore_signal(barrier, inc=1, device_id={"reg": lax.rem(me + o, n)}, device_id_type=MESH)
-    pl.semaphore_wait(barrier, n - 1)
-
-    def send(t):
+    def greet(sem):
+        for dy, dx in ORDER[:4]:
+            there = lax.rem(y + dy, side) * side + lax.rem(x + dx, side)
+            pl.semaphore_signal(sem, inc=1, device_id={"reg": there}, device_id_type=MESH)
+        pl.semaphore_wait(sem, 4)
+
+    greet(pltpu.get_barrier_semaphore())
+
+    def send(t, greeting=False):
         pltpu.make_async_copy(args[t], stage.at[t], load_sem.at[t]).wait()
         for dy, dx in ORDER:
+            if greeting and (dy, dx) in FURTHER:
+                greet(greet_sem.at[FURTHER.index((dy, dx))])
             yy, xx = lax.rem(y + dy, side), lax.rem(x + dx, side)
             takes, head = role(yy, xx)
             takes = jnp.logical_or(takes, yy // 2 == part)
@@ -128,7 +134,7 @@
         def _():
             wait(frecv_sem.at[t // 2], half)
 
-    send(KS)
+    send(KS, greeting=True)
     send(Q)
     sent(KS)
     send(KN)
@@ -203,8 +209,7 @@
     def tile(r):
         return (osum[r] + jnp.dot(pn[r], around(in_vn, r), preferred_element_type=jnp.float32)).astype(jnp.bfloat16)
 
-    def finish(o, _):
-        r = first + lax.rem(me - first + o, count)
+    def give(r):
         outbox[r] = tile(r)
         pltpu.make_async_remote_copy(
             src_ref=outbox.at[r],
@@ -214,6 +219,18 @@
             device_id={"reg": r},
             device_id_type=MESH,
         ).start()
+
+    @pl.when(jnp.logical_and(first == 0, me != 0))
+    def _():
+        give(0)
+
+    def finish(o, _):
+        r = first + lax.rem(me - first + o, count)
+
+        @pl.when(r != 0)
+        def _():
+            give(r)
+
         return 0
 
     lax.fori_loop(1, count, finish, 0)
@@ -260,7 +277,7 @@
                 pltpu.VMEM((n, rows, HD), jnp.float32),
                 pltpu.VMEM((n, rows, HD), jnp.float32),
                 pltpu.VMEM((n, rows, HD), jnp.bfloat16),
-                dma((5,)), dma((5,)), dma((5,)), dma((2,)), dma((2,)), dma, dma,
+                dma((5,)), dma((5,)), dma((5,)), dma((2,)), dma((2,)), dma, dma, pltpu.SemaphoreType.REGULAR((3,)),
             ],
             compiler_params=pltpu.CompilerParams(collective_id=0, has_side_effects=True, vmem_limit_bytes=20 << 20),
         )(pltpu.with_memory_space_constraint(neighbours.T, pltpu.HBM), *[pltpu.with_memory_space_constraint(a, pltpu.HBM) for a in (queries, keys_stale, keys_now, values_stale, values_now)])

time: 42.2 us -> 40.2 us (0.953)
  the two profiles are of different devices: /device:TPU:192 before, /device:TPU:72 now
where the time goes in v4:
time: 40.2 us; the launch traced here: 40.1 us
  Pallas kernels  39.3 us (98%)
  local copies, waits for them, and re-layouts  0.75 us (2%)
    pallas_call x1, Pallas kernels, on_device(): pl.pallas_call(functools.partial(kernel, side, slots), out_shape=jax.Shap...  39.3 us

profile of v4, /device:TPU:72, one launch (start us, length us, event | category | flops | bytes accessed | tf_op | source)
XLA Modules:
  0.0 40.1 jit_solution(7517681815821634709)
XLA Ops:
  0.0 39.3 %shard_map.64 = bf16[128,1536]{1,0:T(8,128)(2,1)S(1)} custom-call(s32[8,16]{1,0:T(8,128)} %bitcast.1, bf16[128,1536]{1,0:T(8,128)(2,1)} %q_ref.1, bf16[128,1536]{1,0:T(8,128)(2,1)} %ks_ref.1, bf16[128,1536]{1,0:T(8,128)(2,1)} %kn_ref.1, bf16[128,1536]{1,0:T(8,128)(2,1)} %vs_ref.1, bf16[128,1536]{1,0:T(8,128)(2,1)} %vn_ref.1), custom_call_target="tpu_custom_call" | custom-call | tf_op jit(solution)/shard_map/pallas_call | solution.py:266
  39.3 0.7 %copy.8 = bf16[128,1536]{1,0:T(8,128)(2,1)} copy(bf16[128,1536]{1,0:T(8,128)(2,1)S(1)} %shard_map.64) | data formatting | bytes 786432

commit v5 on v4

--- a/solution.py
+++ b/solution.py
@@ -49,18 +49,23 @@
     def cols(h):
         return pl.ds(pl.multiple_of(h * HD, HD), HD)
 
-    for t, ref in enumerate(args):
-        pltpu.make_async_copy(ref, stage.at[t], load_sem.at[t]).start()
-    for t, ref in enumerate(args):
-        pltpu.make_async_copy(ref.at[:, cols(my_head)], inbox[t].at[me], recv_sem.at[t]).start()
-
-    def greet(sem):
+    def hail(sem):
         for dy, dx in ORDER[:4]:
             there = lax.rem(y + dy, side) * side + lax.rem(x + dx, side)
             pl.semaphore_signal(sem, inc=1, device_id={"reg": there}, device_id_type=MESH)
+
+    def greet(sem):
+        hail(sem)
         pl.semaphore_wait(sem, 4)
 
-    greet(pltpu.get_barrier_semaphore())
+    barrier = pltpu.get_barrier_semaphore()
+    hail(barrier)
+    for t in (KS, Q, KN, VS, VN):
+        pltpu.make_async_copy(args[t], stage.at[t], load_sem.at[t]).start()
+    for t, ref in enumerate(args):
+        pltpu.make_async_copy(ref.at[:, cols(my_head)], inbox[t].at[me], recv_sem.at[t]).start()
+
+    pl.semaphore_wait(barrier, 4)
 
     def send(t, greeting=False):
         pltpu.make_async_copy(args[t], stage.at[t], load_sem.at[t]).wait()
@@ -137,10 +142,10 @@
     send(KS, greeting=True)
     send(Q)
     sent(KS)
-    send(KN)
+    send(VS)
     pass_on(KS)
     sent(Q)
-    send(VS)
+    send(KN)
     arrived(Q)
     passed(KS)
 
@@ -171,9 +176,9 @@
         return weights.astype(jnp.bfloat16), jnp.broadcast_to(peak, (rows, HD)), jnp.broadcast_to(total, (rows, HD))
 
     each(stale_scores, ps, mb, lb)
-    sent(KN)
     send(VN)
     pass_on(VS)
+    sent(KN)
     arrived(KN)
 
     def around(ref, r):

time: 40.2 us -> 39.9 us (level)
    pallas_call x1, Pallas kernels: 39.3 us -> 38.9 us  [on_device(): pl.pallas_call(functools.partial(kernel, side, slots), out_shape=jax.Shap...]
where the time goes in v5:
time: 39.9 us; the launch traced here: 39.6 us
  Pallas kernels  38.9 us (97%)
  local copies, waits for them, and re-layouts  0.75 us (2%)
    pallas_call x1, Pallas kernels, on_device(): pl.pallas_call(functools.partial(kernel, side, slots), out_shape=jax.Shap...  38.9 us

profile of v5, /device:TPU:72, one launch (start us, length us, event | category | flops | bytes accessed | tf_op | source)
XLA Modules:
  0.0 39.6 jit_solution(4897572181618160990)
XLA Ops:
  0.0 38.9 %shard_map.64 = bf16[128,1536]{1,0:T(8,128)(2,1)S(1)} custom-call(s32[8,16]{1,0:T(8,128)} %bitcast.1, bf16[128,1536]{1,0:T(8,128)(2,1)} %q_ref.1, bf16[128,1536]{1,0:T(8,128)(2,1)} %ks_ref.1, bf16[128,1536]{1,0:T(8,128)(2,1)} %kn_ref.1, bf16[128,1536]{1,0:T(8,128)(2,1)} %vs_ref.1, bf16[128,1536]{1,0:T(8,128)(2,1)} %vn_ref.1), custom_call_target="tpu_custom_call" | custom-call | tf_op jit(solution)/shard_map/pallas_call | solution.py:271
  38.9 0.7 %copy.8 = bf16[128,1536]{1,0:T(8,128)(2,1)} copy(bf16[128,1536]{1,0:T(8,128)(2,1)S(1)} %shard_map.64) | data formatting | bytes 786432

commit v6 on v5

--- a/solution.py
+++ b/solution.py
@@ -11,7 +11,7 @@
 MESH = pl.DeviceIdType.MESH
 LOG2E = 1.4426950408889634
 LOW = -1e30
-GROUP = 4
+GROUP = 8
 Q, KS, KN, VS, VN = range(5)
 ORDER = (
     (0, 1), (0, 3), (1, 0), (3, 0), (1, 1), (3, 3), (1, 3), (3, 1),

time: 39.9 us -> 39.9 us (level)
  no operation moved by 1% of the time
where the time goes in v6:
time: 39.9 us; the launch traced here: 39.5 us
  Pallas kernels  38.7 us (97%)
  local copies, waits for them, and re-layouts  0.75 us (2%)
    pallas_call x1, Pallas kernels, on_device(): pl.pallas_call(functools.partial(kernel, side, slots), out_shape=jax.Shap...  38.7 us

profile of v6, /device:TPU:72, one launch (start us, length us, event | category | flops | bytes accessed | tf_op | source)
XLA Modules:
  0.0 39.5 jit_solution(16465929071011499186)
XLA Ops:
  0.0 38.7 %shard_map.64 = bf16[128,1536]{1,0:T(8,128)(2,1)S(1)} custom-call(s32[8,16]{1,0:T(8,128)} %bitcast.1, bf16[128,1536]{1,0:T(8,128)(2,1)} %q_ref.1, bf16[128,1536]{1,0:T(8,128)(2,1)} %ks_ref.1, bf16[128,1536]{1,0:T(8,128)(2,1)} %kn_ref.1, bf16[128,1536]{1,0:T(8,128)(2,1)} %vs_ref.1, bf16[128,1536]{1,0:T(8,128)(2,1)} %vn_ref.1), custom_call_target="tpu_custom_call" | custom-call | tf_op jit(solution)/shard_map/pallas_call | solution.py:271
  38.7 0.7 %copy.8 = bf16[128,1536]{1,0:T(8,128)(2,1)} copy(bf16[128,1536]{1,0:T(8,128)(2,1)S(1)} %shard_map.64) | data formatting | bytes 786432
